TPU v7x, 32 devices: a whole 2x2x4 slice. The times are simulated.
32 devices in a mesh: face: 16 (over z, y, core), sub: 2 (over x).
Axes of the slice: x: 2, y: 2, z: 4, core: 2. Of those that a mesh axis runs over, the one named last changes fastest.
Arguments:
- prognostic: bfloat16 [3, 2048, 16, 128], P(None, ('face', 'sub')), may hold values from -4 to 4
- metric: float32 [4, 2048, 16], P(None, ('face', 'sub')), may hold values from -0.35 to 1.6, as said below
- coriolis: float32 [2048, 16], P(('face', 'sub')), may hold values from -1.5 to 1.5
- node_point: int32 [2048, 16], P(('face', 'sub')), may hold values from 0 to 678, as said below
- send_point: int32 [6784], P(('face', 'sub')), may hold values from 0 to 678, as said below
- recv_point: int32 [6784], P(('face', 'sub')), may hold values from 0 to 678, as said below
Outputs:
- advanced: bfloat16 [3, 2048, 16, 128], P(None, ('face', 'sub'))
Inputs may be any that keep to these rules, and one draw needn't show every extreme that they name: `node_point`: each device's numbers are its 679 local points; element nodes that are the same point of the surface on one device carry the same number. `send_point`: on every device the 212 slots form groups in this order: 7 slots of offset +1, 7 of offset -1, 97 of offset +8, 97 of offset -8, then one slot each of offsets 8 + 1, -8 - 1, 7, 1 - 8. A slot names the sender's point that the device at curve index d + o, taken modulo 32, shares. Every slot is used. `recv_point`: slot s of device d names the local point that is the same surface point as the sender's slot s, the sender being the device at d minus the slot's group offset modulo 32. The copies of every shared point are linked between every two devices that hold them. `metric`: entries 0 and 3 lie in [0.6, 1.6], entries 1 and 2 in [-0.35, 0.35].
All inputs are finite; a program needn't handle non-finite values.
Results may differ from a plain program's by a relative error of at most 0.007.
Values sent between devices are 32-bit elements; how exact they have to be, the bound alone decides.
A program may use at most 64 MiB of HBM per device.

v0:
```python
import functools
import math

import jax
import jax.numpy as jnp
import numpy as np
from jax import lax
from jax.experimental import pallas as pl
from jax.experimental.pallas import tpu as pltpu
from jax.sharding import PartitionSpec as P

BX = 32
BY = 2
STEP_SIZE = 0.1
ROWS = 256
LANES = 128
F32 = jnp.float32
BF16 = jnp.bfloat16
MESH = pl.DeviceIdType.MESH


def gll_tables():
    abscissa = np.array([-1.0, -math.sqrt(0.2), math.sqrt(0.2), 1.0])
    legendre = 0.5 * (5.0 * abscissa * abscissa * abscissa - 3.0 * abscissa)
    derivative = np.zeros((4, 4))
    for target in range(4):
        for source in range(4):
            if target != source:
                derivative[target, source] = legendre[target] / (
                    legendre[source] * (abscissa[target] - abscissa[source])
                )
    derivative[0, 0] = -3.0
    derivative[3, 3] = 3.0
    weights = np.array([1.0, 5.0, 5.0, 1.0]) / 6.0
    return (derivative, weights)


def round_bf16(values):
    return np.asarray(values, dtype=jnp.bfloat16).astype(np.float64)


def operator_tables():
    derivative, weights = gll_tables()
    eye4 = np.eye(4)
    node_weight = np.kron(weights, weights)
    along_c = node_weight[:, None] * np.kron(eye4, derivative)
    along_r = node_weight[:, None] * np.kron(derivative, eye4)
    best = None
    for trial in np.linspace(1.0, 2.0, 2001)[:-1]:
        error = max(
            np.max(np.abs(round_bf16(trial * t) / trial - t) / (np.abs(t).max(1, keepdims=True)))
            for t in (along_c, along_r)
        )
        if best is None or error < best[0]:
            best = (error, trial)
    scale = float(best[1])
    eye = np.eye(ROWS // 16)
    stacked = np.concatenate([np.kron(eye, along_c), np.kron(eye, along_r)], axis=0) * scale
    return np.asarray(stacked, dtype=np.float32), scale


def link_groups(lap_blocks):
    side_points = 3 * BY + 1
    top_points = 3 * BX + 1
    group_sizes = [
        (1, side_points),
        (-1, side_points),
        (lap_blocks, top_points),
        (-lap_blocks, top_points),
        (lap_blocks + 1, 1),
        (-lap_blocks - 1, 1),
        (lap_blocks - 1, 1),
        (1 - lap_blocks, 1),
    ]
    groups = []
    first_slot = 0
    first_row = 0
    for offset, slot_count in group_sizes:
        padded = -(-slot_count // 8) * 8
        groups.append((offset, first_slot, slot_count, first_row, padded))
        first_slot += slot_count
        first_row += padded
    return groups, first_row


def iota(shape, dim):
    return lax.broadcasted_iota(jnp.int32, shape, dim)


def dot(a, b):
    return lax.dot_general(a, b, (((1,), (0,)), ((), ())), preferred_element_type=F32)


def dot_nt(a, b):
    return lax.dot_general(a, b, (((1,), (1,)), ((), ())), preferred_element_type=F32)


def wait_bytes(ref, sem):
    pltpu.make_async_copy(ref, ref, sem).wait()


def kernel(
    sizes, groups, slots, scale,
    prog_hbm, metric_hbm, cor_hbm, node_hbm, send_hbm, recv_hbm, ops_hbm,
    out_hbm,
    prog, metric, cor, node, sendp, recvp, ops,
    wide, weighted, summed, inverse, table_s, table_r,
    outgoing, arrived, out_mass, arrived_mass,
    in_sem, send_sem, recv_sem, msend_sem, mrecv_sem,
):
    nface, nsub = sizes
    total = nface * nsub
    nodes = prog.shape[1]
    blocks = nodes // ROWS
    me = lax.axis_index("face") * nsub + lax.axis_index("sub")
    peers = []
    for offset, *_ in groups:
        other = lax.rem(me + (offset % total), total)
        peers.append((other // nsub, lax.rem(other, nsub)))

    arrived[...] = jnp.zeros_like(arrived)
    barrier = pltpu.get_barrier_semaphore()
    for peer in peers:
        pl.semaphore_signal(barrier, inc=1, device_id=peer, device_id_type=MESH)

    loads = []
    for k, (src, dst) in enumerate((
        (metric_hbm, metric), (cor_hbm, cor), (node_hbm, node),
        (send_hbm, sendp), (recv_hbm, recvp), (prog_hbm, prog), (ops_hbm, ops),
    )):
        copy = pltpu.make_async_copy(src, dst, in_sem.at[k])
        copy.start()
        loads.append(copy)
    for copy in loads[:5]:
        copy.wait()

    elements = node.shape[1]
    a, b, e, g = metric[0], metric[1], metric[2], metric[3]
    inv_det = 1.0 / (a * g - b * e)
    lane16 = iota((16, 1), 0)
    col, row = lane16 & 3, lane16 >> 2
    w_node = jnp.where((col == 0) | (col == 3), 1 / 6, 5 / 6) * jnp.where((row == 0) | (row == 3), 1 / 6, 5 / 6)
    mass = w_node * inv_det
    compact = jnp.concatenate(
        [a * inv_det, b * inv_det, e * inv_det, g * inv_det, scale * (mass * cor[...]), mass,
         node[...].astype(F32), jnp.zeros((16, elements), F32)], axis=0).T
    upper = compact.astype(BF16).astype(F32)
    both = jnp.concatenate([upper, compact - upper], axis=1)
    own = (iota((16, 2 * LANES), 1) & 15) == iota((16, 2 * LANES), 0)
    spread = jnp.where(own[None], jnp.broadcast_to(both[:, None, :], (elements, 16, 2 * LANES)), 0.0)
    spread = spread.reshape(nodes, 2 * LANES).astype(BF16)
    pick_l = (iota((2 * LANES, 7 * LANES), 0) & (LANES - 1)) >> 4
    pick = (pick_l == (iota((2 * LANES, 7 * LANES), 1) >> 7)).astype(F32).astype(BF16)
    row_l = (iota((8, 2 * LANES), 1) & (LANES - 1)) >> 4
    point_row = dot_nt((row_l == 6).astype(F32).astype(BF16), spread)[0:1]
    mass_row = dot_nt((row_l == 5).astype(F32).astype(BF16), spread).astype(BF16)
    wide[...] = dot(spread, pick)
    weighted[:, 3 * LANES:] = wide[:, 5 * LANES:6 * LANES].astype(BF16)

    count = sendp.shape[1]
    padded = iota((slots, 1), 0)
    slot_of = jnp.full((slots, 1), -1, jnp.int32)
    for _, first_slot, slot_count, first_row, _ in groups:
        inside = (padded >= first_row) & (padded < first_row + slot_count)
        slot_of = jnp.where(inside, padded - first_row + first_slot, slot_of)
    chosen = slot_of == iota((slots, count), 1)
    vacant = jnp.where(slot_of < 0, -1.0, 0.0)
    send_col = jnp.sum(jnp.where(chosen, sendp[...].astype(F32), 0.0), axis=1, keepdims=True) + vacant
    recv_col = jnp.sum(jnp.where(chosen, recvp[...].astype(F32), 0.0), axis=1, keepdims=True) + vacant
    same = iota((slots, slots), 0) == iota((slots, slots), 1)
    recv_row = jnp.sum(jnp.where(same, recv_col, 0.0), axis=0, keepdims=True)
    table_s[...] = jnp.where(send_col == point_row, 1.0, 0.0).astype(BF16)
    out_mass[...] = dot_nt(mass_row, table_s[...])[0:1]

    pl.semaphore_wait(barrier, len(peers))
    for k in range(len(groups)):
        copy = pltpu.make_async_remote_copy(
            src_ref=out_mass, dst_ref=arrived_mass.at[k],
            send_sem=msend_sem.at[0], recv_sem=mrecv_sem.at[0],
            device_id=peers[k], device_id_type=MESH)
        copy.start()
    order = [k for k in range(len(groups)) if k not in (2, 3)] + [2, 3]

    def field_copy(field, k):
        used, first_row = groups[k][2], groups[k][3]
        return pltpu.make_async_remote_copy(
            src_ref=outgoing.at[field, pl.ds(first_row, used)],
            dst_ref=arrived.at[field, pl.ds(first_row, used)],
            send_sem=send_sem.at[field], recv_sem=recv_sem.at[field],
            device_id=peers[k], device_id_type=MESH)

    def send_field(field):
        for k in order:
            field_copy(field, k).start()

    loads[5].wait()
    loads[6].wait()
    along_c = ops[:ROWS]
    along_r = ops[ROWS:]

    def read(block):
        rows = pl.ds(block * ROWS, ROWS)
        fields = [prog[f, rows].astype(F32) for f in range(3)]
        coefs = [wide[rows, k * LANES:(k + 1) * LANES] for k in range(5)]
        return rows, fields, coefs

    for pair in range(0, blocks, 2):
        one, two = [], []
        for block in (pair, pair + 1):
            _, (u1, u2, phi), (ca, cb, ce, cg, _) = read(block)
            one.append((phi * (ca * u1 + cb * u2)).astype(BF16))
            two.append((phi * (ce * u1 + cg * u2)).astype(BF16))
        div = dot(along_c, jnp.concatenate(one, axis=1)) + dot(along_r, jnp.concatenate(two, axis=1))
        for j, block in enumerate((pair, pair + 1)):
            weighted[pl.ds(block * ROWS, ROWS), 2 * LANES:3 * LANES] = (
                -div[:, j * LANES:(j + 1) * LANES]).astype(BF16)
    outgoing[2] = dot(table_s[...], weighted[:, 2 * LANES:3 * LANES])
    send_field(2)

    for pair in range(0, blocks, 2):
        one, two, energy = [], [], []
        for block in (pair, pair + 1):
            _, (u1, u2, phi), (ca, cb, ce, cg, _) = read(block)
            one.append((ca * u2 - cb * u1).astype(BF16))
            two.append((ce * u2 - cg * u1).astype(BF16))
            energy.append((0.5 * (u1 * u1 + u2 * u2) + phi).astype(BF16))
        energy = jnp.concatenate(energy, axis=1)
        vort = dot(along_c, jnp.concatenate(one, axis=1)) + dot(along_r, jnp.concatenate(two, axis=1))
        ref1 = dot(along_c, energy)
        ref2 = dot(along_r, energy)
        for j, block in enumerate((pair, pair + 1)):
            rows, (u1, u2, _), (ca, cb, ce, cg, cf) = read(block)
            lanes = slice(j * LANES, (j + 1) * LANES)
            eta = vort[:, lanes] + cf
            x1, x2 = ref1[:, lanes], ref2[:, lanes]
            weighted[rows, 0:LANES] = (eta * u2 - (ca * x1 + ce * x2)).astype(BF16)
            weighted[rows, LANES:2 * LANES] = (-(eta * u1) - (cb * x1 + cg * x2)).astype(BF16)
    pair_out = dot(table_s[...], weighted[:, 0:2 * LANES])
    outgoing[0] = pair_out[:, :LANES]
    outgoing[1] = pair_out[:, LANES:]
    send_field(0)
    send_field(1)

    for block in range(blocks):
        rows = pl.ds(block * ROWS, ROWS)
        point = wide[rows, 6 * LANES:7 * LANES][:, 0:1]
        meet = jnp.where(point == point_row, 1.0, 0.0).astype(BF16)
        summed[rows, :] = dot(meet, weighted[...])

    wait_bytes(arrived_mass, mrecv_sem.at[0])
    lane = iota((1, slots), 1)
    mass_in = jnp.zeros((1, slots), F32)
    for k, (_, _, _, first_row, size) in enumerate(groups):
        inside = (lane >= first_row) & (lane < first_row + size)
        mass_in = jnp.where(inside, arrived_mass[k, 0:1, :], mass_in)
    ones = jnp.ones((slots, LANES), BF16)
    for block in range(blocks):
        rows = pl.ds(block * ROWS, ROWS)
        point = wide[rows, 6 * LANES:7 * LANES][:, 0:1]
        hit = point == recv_row
        table_r[rows, :] = jnp.where(hit, 1.0, 0.0).astype(BF16)
        far = dot(jnp.where(hit, mass_in, 0.0).astype(BF16), ones)
        inv = (STEP_SIZE / scale) / (summed[rows, 3 * LANES:] + far)
        inverse[rows, :] = inv
        for f in range(3):
            lanes = slice(f * LANES, (f + 1) * LANES)
            summed[rows, lanes] = prog[f, rows].astype(F32) + inv * summed[rows, lanes]

    for f in (2, 0, 1):
        wait_bytes(arrived.at[f, pl.ds(0, count)], recv_sem.at[f])
        landed = arrived[f].astype(BF16)
        for block in range(blocks):
            rows = pl.ds(block * ROWS, ROWS)
            far = dot(table_r[rows, :], landed)
            value = summed[rows, f * LANES:(f + 1) * LANES] + inverse[rows, :] * far
            out_hbm[f, rows] = value
    wait_bytes(arrived_mass, msend_sem.at[0])
    for f in range(3):
        wait_bytes(outgoing.at[f, pl.ds(0, count)], send_sem.at[f])


def local(prognostic, metric, coriolis, node_point, send_point, recv_point):
    elements, per, levels = prognostic.shape[1:]
    nodes = elements * per
    sizes = (lax.axis_size("face"), lax.axis_size("sub"))
    groups, slots = link_groups(4 * sizes[1])
    tables, scale = operator_tables()
    links = send_point.shape[0]
    any_spec = pl.BlockSpec(memory_space=pltpu.HBM)
    dma = pltpu.SemaphoreType.DMA
    vmem = pltpu.VMEM
    out = pl.pallas_call(
        functools.partial(kernel, sizes, groups, slots, scale),
        out_shape=pltpu.VMEM((3, nodes, levels), F32),
        in_specs=[any_spec] * 7,
        out_specs=pl.BlockSpec(memory_space=pltpu.VMEM),
        scratch_shapes=[
            vmem((3, nodes, levels), BF16),
            vmem((4, per, elements), F32),
            vmem((per, elements), F32),
            vmem((per, elements), jnp.int32),
            vmem((1, links), jnp.int32),
            vmem((1, links), jnp.int32),
            vmem((2 * ROWS, ROWS), BF16),
            vmem((nodes, 7 * LANES), F32),
            vmem((nodes, 4 * LANES), BF16),
            vmem((nodes, 4 * LANES), F32),
            vmem((nodes, LANES), F32),
            vmem((slots, nodes), BF16),
            vmem((nodes, slots), BF16),
            vmem((3, slots, levels), F32),
            vmem((3, slots, levels), F32),
            vmem((1, slots), F32),
            vmem((len(groups), 1, slots), F32),
            dma((7,)),
            dma((3,)),
            dma((3,)),
            dma((1,)),
            dma((1,)),
        ],
        compiler_params=pltpu.CompilerParams(
            collective_id=0, has_side_effects=True),
    )(
        prognostic.reshape(3, nodes, levels), metric.swapaxes(1, 2), coriolis.T, node_point.T,
        send_point.reshape(1, links), recv_point.reshape(1, links),
        jnp.asarray(tables, dtype=BF16),
    )
    return out.astype(BF16).reshape(3, elements, per, levels)


def solution(mesh):
    placed = (
        P(None, ("face", "sub"), None, None),
        P(None, ("face", "sub"), None),
        P(("face", "sub"), None),
        P(("face", "sub"), None),
        P(("face", "sub")),
        P(("face", "sub")),
    )
    return jax.shard_map(
        local,
        mesh=mesh,
        in_specs=placed,
        out_specs=P(None, ("face", "sub"), None, None),
        check_vma=False,
    )
```

profile of v0, /device:TPU:0, one launch (start us, length us, event | category | flops | bytes accessed | tf_op | source)
XLA Modules:
  0.0 16.4 jit_solution(12627563905529443250)
XLA Ops:
  0.0 15.4 %shard_map.73 = f32[3,1024,128]{2,1,0:T(8,128)S(1)} custom-call(bf16[3,1024,128]{2,1,0:T(8,128)(2,1)} %bitcast.7, f32[4,16,64]{2,1,0:T(8,128)} %bitcast.8, f32[16,64]{1,0:T(8,128)} %bitcast.9, s32[16,64]{1,0:T(8,128)} %bitcast.10, s32[1,212]{1,0:T(1,128)} %bitcast.11, s32[1,212]{1,0:T(1,128)} %bitcast.12, bf16[512,256]{1,0:T(8,128)(2,1)} %constant.2.clone.ops_hbm), custom_call_target="tpu_custom_call" | custom-call | tf_op jit(solution)/shard_map/pallas_call | solution.py:292
  15.4 1.0 %convert_element_type.3 = bf16[3,1024,128]{2,1,0:T(8,128)(2,1)} convert(f32[3,1024,128]{2,1,0:T(8,128)S(1)} %shard_map.73) | non-fusion elementwise | flops 393216 | bytes 2359296 | tf_op jit(solution)/shard_map/convert_element_type | solution.py:328
where the time goes:
time: 16.5 us; the launch traced here: 16.4 us
  Pallas kernels  15.4 us (93%)
  other arithmetic  0.98 us (6%)
    pallas_call x1, Pallas kernels, local(): pl.pallas_call(functools.partial(kernel, sizes, groups, slots, scale), ou...  15.4 us
    convert_element_type x1, other arithmetic, local(): return out.astype(BF16).reshape(3, elements, per, levels)  0.98 us

commit v1 on v0

v1 whole, which is shorter than its diff:
```python
import functools
import math

import jax
import jax.numpy as jnp
import numpy as np
from jax import lax
from jax.experimental import pallas as pl
from jax.experimental.pallas import tpu as pltpu
from jax.sharding import PartitionSpec as P

BX = 32
BY = 2
STEP_SIZE = 0.1
ROWS = 256
BAND = 128
LANES = 128
BULK = (2, 3)
SMALL = (0, 1, 4, 5, 6, 7)
F32 = jnp.float32
BF16 = jnp.bfloat16
MESH = pl.DeviceIdType.MESH


def gll_tables():
    abscissa = np.array([-1.0, -math.sqrt(0.2), math.sqrt(0.2), 1.0])
    legendre = 0.5 * (5.0 * abscissa * abscissa * abscissa - 3.0 * abscissa)
    derivative = np.zeros((4, 4))
    for target in range(4):
        for source in range(4):
            if target != source:
                derivative[target, source] = legendre[target] / (
                    legendre[source] * (abscissa[target] - abscissa[source])
                )
    derivative[0, 0] = -3.0
    derivative[3, 3] = 3.0
    weights = np.array([1.0, 5.0, 5.0, 1.0]) / 6.0
    return (derivative, weights)


def round_bf16(values):
    return np.asarray(values, dtype=jnp.bfloat16).astype(np.float64)


def operator_tables():
    derivative, weights = gll_tables()
    eye4 = np.eye(4)
    node_weight = np.kron(weights, weights)
    along_c = node_weight[:, None] * np.kron(eye4, derivative)
    along_r = node_weight[:, None] * np.kron(derivative, eye4)
    best = None
    for trial in np.linspace(1.0, 2.0, 2001)[:-1]:
        error = max(
            np.max(np.abs(round_bf16(trial * t) / trial - t) / (np.abs(t).max(1, keepdims=True)))
            for t in (along_c, along_r)
        )
        if best is None or error < best[0]:
            best = (error, trial)
    scale = float(best[1])
    tiles = [np.tile(t, (1, BAND // 16)) for t in (along_c, along_r)]
    stacked = np.concatenate(tiles, axis=0) * scale
    return np.asarray(stacked, dtype=np.float32), scale


def link_groups(lap_blocks):
    side_points = 3 * BY + 1
    top_points = 3 * BX + 1
    group_sizes = [
        (1, side_points),
        (-1, side_points),
        (lap_blocks, top_points),
        (-lap_blocks, top_points),
        (lap_blocks + 1, 1),
        (-lap_blocks - 1, 1),
        (lap_blocks - 1, 1),
        (1 - lap_blocks, 1),
    ]
    starts = [0]
    for _, slot_count in group_sizes:
        starts.append(starts[-1] + slot_count)
    groups = [None] * len(group_sizes)
    first_row = 0
    for k in (0, 1, 2, 4, 3, 5, 6, 7):
        offset, slot_count = group_sizes[k]
        padded = -(-(slot_count + 1) // 8) * 8
        groups[k] = (offset, starts[k], slot_count, first_row, padded)
        first_row += padded
    return groups, first_row


def iota(shape, dim):
    return lax.broadcasted_iota(jnp.int32, shape, dim)


def dot(a, b):
    return lax.dot_general(a, b, (((1,), (0,)), ((), ())), preferred_element_type=F32)


def dot_nt(a, b):
    return lax.dot_general(a, b, (((1,), (1,)), ((), ())), preferred_element_type=F32)


def wait_bytes(ref, sem):
    pltpu.make_async_copy(ref, ref, sem).wait()


def kernel(
    sizes, groups, slots, scale,
    prog_hbm, metric_hbm, cor_hbm, node_hbm, send_hbm, recv_hbm, ops_hbm,
    out_hbm,
    prog, metric, cor, node, sendp, recvp, ops,
    wide, weighted, summed, inverse, table_s, table_r,
    expand, pick, spread, vort, slim,
    outgoing, arrived, in_sem, send_sem, recv_sem, ready, mark,
):
    nface, nsub = sizes
    total = nface * nsub
    nodes = prog.shape[1]
    blocks = nodes // ROWS
    elements = node.shape[1]

    def load(src, dst, k):
        copy = pltpu.make_async_copy(src, dst, in_sem.at[k])
        copy.start()
        return copy

    loads = [load(src, dst, k) for k, (src, dst) in enumerate((
        (metric_hbm, metric), (cor_hbm, cor), (node_hbm, node),
        (send_hbm, sendp), (recv_hbm, recvp), (ops_hbm, ops)))]
    fields = [load(prog_hbm.at[f], prog.at[f], len(loads) + f) for f in range(3)]

    pl.semaphore_signal(mark, 1)
    me = lax.axis_index("face") * nsub + lax.axis_index("sub")
    lap = 4 * nsub

    def rank(index):
        hops = 4 * (index // lap) + lax.rem(index, lap) // (2 * nsub) + lax.rem(index, nsub)
        return hops * total + index

    peers, lower, first_lap = [], [], []
    for offset, *_ in groups:
        other = lax.rem(me + (offset % total), total)
        peers.append((other // nsub, lax.rem(other, nsub)))
        lower.append(rank(other) < rank(me))
        first_lap.append(other < lap)
    higher = [jnp.logical_not(flag) for flag in lower]
    middle = lower[3] & higher[2]

    barrier = pltpu.get_barrier_semaphore()
    for k, peer in enumerate(peers):
        @pl.when(higher[k])
        def _(peer=peer):
            pl.semaphore_signal(barrier, inc=1, device_id=peer, device_id_type=MESH)
    for k, (_, _, used, first_row, padded) in enumerate(groups):
        if k in BULK:
            gap = pl.ds(first_row + used, padded - used)
            arrived[0:2, gap] = jnp.zeros((2, padded - used, arrived.shape[2]), F32)
        if padded > used + 1:
            gap = pl.ds(first_row + used + 1, padded - used - 1)
            part = slice(2, 3) if k in BULK else slice(0, 3)
            arrived[part, gap] = jnp.zeros((part.stop - part.start, padded - used - 1, arrived.shape[2]), F32)

    expand[...] = jnp.where(
        iota((elements, nodes), 0) == iota((elements, nodes), 1) >> 4, 1.0, 0.0).astype(BF16)
    pick_l = (iota((LANES, 3 * LANES), 0) & (LANES // 2 - 1)) >> 4
    pick[...] = jnp.where(pick_l == (iota((LANES, 3 * LANES), 1) >> 7), 1.0, 0.0).astype(BF16)
    for copy in loads:
        copy.wait()

    a, b, e, g = metric[0], metric[1], metric[2], metric[3]
    inv_det = 1.0 / (a * g - b * e)
    lane16 = iota((16, 1), 0)
    col, row = lane16 & 3, lane16 >> 2
    w_node = jnp.where((col == 0) | (col == 3), 1 / 6, 5 / 6) * jnp.where((row == 0) | (row == 3), 1 / 6, 5 / 6)
    mass = w_node * inv_det
    parts = [a * inv_det, b * inv_det, e * inv_det, g * inv_det, node[...].astype(F32)]
    stack = jnp.concatenate(parts, axis=0)
    upper = stack.astype(BF16)
    rest = (stack - upper.astype(F32)).astype(BF16)
    spans = dot(jnp.concatenate([upper, rest], axis=0), expand[...])
    half = stack.shape[0]
    spans = spans[:half] + spans[half:]
    own_row = (iota((16, nodes), 1) & 15) == iota((16, nodes), 0)
    row_a, row_b, row_e, row_g, point_row = [
        jnp.sum(jnp.where(own_row, spans[16 * k:16 * k + 16], 0.0), axis=0, keepdims=True) for k in range(5)]

    stack = jnp.concatenate([scale * (mass * cor[...]), mass, parts[4], jnp.zeros_like(mass)], axis=0)
    upper = stack.astype(BF16).astype(F32)
    both = jnp.concatenate([upper, stack - upper], axis=0).T
    own = (iota((16, LANES), 1) & 15) == iota((16, LANES), 0)
    spread[...] = jnp.where(
        own[None], jnp.broadcast_to(both[:, None, :], (elements, 16, LANES)), 0.0
    ).reshape(nodes, LANES).astype(BF16)

    def tile_rows(table):
        return jnp.concatenate([table] * (nodes // BAND), axis=1)

    along_c = tile_rows(ops[0:16, :].astype(F32))
    along_r = tile_rows(ops[16:32, :].astype(F32))
    slim[0:16, :] = (along_c * row_a + along_r * row_e).astype(BF16)
    slim[16:32, :] = (along_c * row_b + along_r * row_g).astype(BF16)
    slim[32:48, :] = (along_c * spans[0:16] + along_r * spans[32:48]).astype(BF16)
    slim[48:64, :] = (along_c * spans[16:32] + along_r * spans[48:64]).astype(BF16)

    count = sendp.shape[1]
    padded = iota((slots, 1), 0)
    slot_of = jnp.full((slots, 1), -1, jnp.int32)
    for _, first_slot, slot_count, first_row, _ in groups:
        inside = (padded >= first_row) & (padded < first_row + slot_count)
        slot_of = jnp.where(inside, padded - first_row + first_slot, slot_of)
    chosen = slot_of == iota((slots, count), 1)
    vacant = jnp.where(slot_of < 0, -1.0, 0.0)
    send_col = jnp.sum(jnp.where(chosen, sendp[...].astype(F32), 0.0), axis=1, keepdims=True) + vacant
    sign = jnp.where(iota((1, nodes), 1) < nodes // 2, 1.0, -1.0)
    table_s[...] = jnp.where(send_col == point_row, sign, 0.0).astype(BF16)

    for part in range(2):
        rows = pl.ds(part * (nodes // 2), nodes // 2)
        first = dot(spread[rows], pick[:, :2 * LANES])
        wide[0, rows] = first[:, :LANES]
        weighted[3, rows] = first[:, LANES:].astype(BF16)

    for copy in fields:
        copy.wait()

    diagonal = jnp.where(iota((BAND, BAND), 0) >> 4 == iota((BAND, BAND), 1) >> 4, 1.0, 0.0).astype(BF16)

    def block(k, here):
        return jnp.concatenate([slim[k:k + 16, here]] * (BAND // 16), axis=0) * diagonal

    for band in range(nodes // BAND):
        rows = pl.ds(band * BAND, BAND)
        here = pl.ds(band * BAND, BAND)
        left = jnp.concatenate([block(k, here) for k in (0, 16)], axis=1)
        u1, u2, phi = prog[0, rows], prog[1, rows], prog[2, rows]
        right = jnp.concatenate([
            jnp.concatenate([u2, phi * u1], axis=1), jnp.concatenate([-u1, phi * u2], axis=1)], axis=0)
        both_terms = dot(left, right)
        vort[rows, :] = both_terms[:, :LANES]
        weighted[2, rows] = (-both_terms[:, LANES:]).astype(BF16)

    def slot_sum(one, two):
        half = nodes // 2
        terms = [
            dot(table_s[:, h * half:(h + 1) * half],
                jnp.concatenate([weighted[one, pl.ds(h * half, half)], weighted[two, pl.ds(h * half, half)]], axis=1))
            for h in range(2)]
        both_fields = terms[0] - terms[1]
        return both_fields[:, :LANES], both_fields[:, LANES:]

    def copy(k, part, extra, sem):
        rows = pl.ds(groups[k][3], groups[k][2] + extra)
        return pltpu.make_async_remote_copy(
            src_ref=outgoing.at[part, rows], dst_ref=arrived.at[part, rows],
            send_sem=send_sem.at[sem], recv_sem=recv_sem.at[sem],
            device_id=peers[k], device_id_type=MESH)

    def one_field(k):
        return copy(k, pl.ds(2, 1), 1, 0)

    def two_fields(k):
        return copy(k, pl.ds(0, 2), 0, 1)

    def all_fields(k):
        return copy(k, pl.ds(0, 3), 1, 2 + SMALL.index(k))

    def early(copies, flag):
        @pl.when(flag)
        def _():
            for item in copies:
                item.start()

    def late(copies, k):
        @pl.when(higher[k])
        def _():
            pl.semaphore_wait(ready.at[k], 1)
            for item in copies:
                item.start()

    near_two, slot_mass = slot_sum(2, 3)
    outgoing[2] = near_two
    place = jnp.where(iota((slots, LANES), 1) == (iota((slots, LANES), 0) & (LANES - 1)), slot_mass, 0.0)
    for _, _, used, first_row, size in groups:
        outgoing[2, first_row + used:first_row + used + 1] = jnp.sum(
            place[first_row:first_row + size], axis=0, keepdims=True)
    waited = sum(flag.astype(jnp.int32) for flag in lower)

    @pl.when(waited > 0)
    def _():
        pl.semaphore_wait(barrier, waited)

    early([one_field(2)], lower[2])
    early([one_field(3)], middle)
    for k, peer in enumerate(peers):
        @pl.when(lower[k])
        def _(k=k, peer=peer):
            pl.semaphore_signal(ready.at[k ^ 1], inc=1, device_id=peer, device_id_type=MESH)

    for band in range(nodes // BAND):
        rows = pl.ds(band * BAND, BAND)
        here = pl.ds(band * BAND, BAND)
        u1, u2, phi = [prog[f, rows].astype(F32) for f in range(3)]
        energy = (0.5 * (u1 * u1 + u2 * u2) + phi).astype(BF16)
        slopes = dot(jnp.concatenate([block(k, here) for k in (32, 48)], axis=0), energy)
        eta = vort[rows, :] + wide[0, rows]
        weighted[0, rows] = (eta * u2 - slopes[:BAND]).astype(BF16)
        weighted[1, rows] = (-(eta * u1) - slopes[BAND:]).astype(BF16)
    near_zero, near_one = slot_sum(0, 1)
    outgoing[0] = near_zero
    outgoing[1] = near_one
    for k in SMALL:
        early([all_fields(k)], lower[k])
    early([two_fields(2)], lower[2])
    early([two_fields(3)], first_lap[3] & lower[3])
    early([one_field(3), two_fields(3)], lower[3] & lower[2])
    late([one_field(2)], 2)
    for k in (0, 6, 4):
        late([all_fields(k)], k)
    early([two_fields(2)], higher[2])

    recv_col = jnp.sum(jnp.where(chosen, recvp[...].astype(F32), 0.0), axis=1, keepdims=True) + vacant
    same = iota((slots, slots), 0) == iota((slots, slots), 1)
    recv_row = jnp.sum(jnp.where(same, recv_col, 0.0), axis=0, keepdims=True)
    wide[1] = dot(spread[...], pick[:, 2 * LANES:])
    all_weighted = jnp.concatenate([weighted[f] for f in range(4)], axis=1)
    for block in range(blocks):
        rows = pl.ds(block * ROWS, ROWS)
        point = wide[1, rows][:, 0:1]
        meet = jnp.where(point == point_row, 1.0, 0.0).astype(BF16)
        summed[rows, :] = dot(meet, all_weighted)

    early([two_fields(3)], middle & jnp.logical_not(first_lap[3]))
    for k in (1, 5, 7, 3):
        late([one_field(k), two_fields(k)] if k in BULK else [all_fields(k)], k)

    def landing(ref, sem):
        rows_one = sum(groups[k][2] + 1 for k in BULK)
        wait_bytes([
            ref.at[pl.ds(2, 1), pl.ds(0, rows_one)],
            ref.at[pl.ds(0, 2), pl.ds(0, rows_one - 2)],
            *(ref.at[pl.ds(0, 3), pl.ds(0, groups[k][2] + 1)] for k in SMALL),
        ][sem], (send_sem if ref is outgoing else recv_sem).at[sem])

    landing(arrived, 0)
    for k in (5, 7, 1, 6, 4, 0):
        landing(arrived, 2 + SMALL.index(k))
    sides = [jnp.zeros((1, LANES), F32)] * (slots // LANES)
    for _, _, used, first_row, _ in groups:
        sides[first_row // LANES] += arrived[2, first_row + used:first_row + used + 1]
    mass_in = jnp.concatenate(sides, axis=1)
    ones = jnp.ones((slots, LANES), BF16)
    for block in range(blocks):
        rows = pl.ds(block * ROWS, ROWS)
        point = wide[1, rows][:, 0:1]
        hit = point == recv_row
        table_r[rows, :] = jnp.where(hit, 1.0, 0.0).astype(BF16)
        far = dot(jnp.where(hit, mass_in, 0.0).astype(BF16), ones)
        inv = (STEP_SIZE / scale) / (summed[rows, 3 * LANES:] + far)
        inverse[rows, :] = inv
        for f in range(3):
            lanes = slice(f * LANES, (f + 1) * LANES)
            summed[rows, lanes] = prog[f, rows].astype(F32) + inv * summed[rows, lanes]

    for sem in range(2, 2 + len(SMALL)):
        landing(outgoing, sem)

    def finish(chosen_fields):
        landed = jnp.concatenate([arrived[f].astype(BF16) for f in chosen_fields], axis=1)
        for block_at in range(blocks):
            rows = pl.ds(block_at * ROWS, ROWS)
            far = dot(table_r[rows, :], landed)
            for j, f in enumerate(chosen_fields):
                value = summed[rows, f * LANES:(f + 1) * LANES] + inverse[rows, :] * far[:, j * LANES:(j + 1) * LANES]
                out_hbm[f, rows] = value.astype(out_hbm.dtype)

    finish([2])
    landing(arrived, 1)
    finish([0, 1])
    for sem in range(2):
        landing(outgoing, sem)
    pl.semaphore_wait(mark, 1)


def local(prognostic, metric, coriolis, node_point, send_point, recv_point):
    elements, per, levels = prognostic.shape[1:]
    nodes = elements * per
    sizes = (lax.axis_size("face"), lax.axis_size("sub"))
    groups, slots = link_groups(4 * sizes[1])
    tables, scale = operator_tables()
    links = send_point.shape[0]
    any_spec = pl.BlockSpec(memory_space=pltpu.HBM)
    dma = pltpu.SemaphoreType.DMA
    vmem = pltpu.VMEM
    out = pl.pallas_call(
        functools.partial(kernel, sizes, groups, slots, scale),
        out_shape=pltpu.VMEM((3, nodes, levels), BF16),
        in_specs=[any_spec] * 7,
        out_specs=pl.BlockSpec(memory_space=pltpu.VMEM),
        scratch_shapes=[
            vmem((3, nodes, levels), BF16),
            vmem((4, per, elements), F32),
            vmem((per, elements), F32),
            vmem((per, elements), jnp.int32),
            vmem((1, links), jnp.int32),
            vmem((1, links), jnp.int32),
            vmem((32, BAND), BF16),
            vmem((2, nodes, LANES), F32),
            vmem((4, nodes, LANES), BF16),
            vmem((nodes, 4 * LANES), F32),
            vmem((nodes, LANES), F32),
            vmem((slots, nodes), BF16),
            vmem((nodes, slots), BF16),
            vmem((elements, nodes), BF16),
            vmem((LANES, 3 * LANES), BF16),
            vmem((nodes, LANES), BF16),
            vmem((nodes, LANES), F32),
            vmem((64, nodes), BF16),
            vmem((3, slots, levels), F32),
            vmem((3, slots, levels), F32),
            dma((9,)),
            dma((2 + len(SMALL),)),
            dma((2 + len(SMALL),)),
            pltpu.SemaphoreType.REGULAR((len(groups),)),
            pltpu.SemaphoreType.REGULAR,
        ],
        compiler_params=pltpu.CompilerParams(
            collective_id=0, has_side_effects=True),
    )(
        prognostic.reshape(3, nodes, levels), metric.swapaxes(1, 2), coriolis.T, node_point.T,
        send_point.reshape(1, links), recv_point.reshape(1, links),
        jnp.asarray(tables, dtype=BF16),
    )
    return out.reshape(3, elements, per, levels)


def solution(mesh):
    placed = (
        P(None, ("face", "sub"), None, None),
        P(None, ("face", "sub"), None),
        P(("face", "sub"), None),
        P(("face", "sub"), None),
        P(("face", "sub")),
        P(("face", "sub")),
    )
    return jax.shard_map(
        local,
        mesh=mesh,
        in_specs=placed,
        out_specs=P(None, ("face", "sub"), None, None),
        check_vma=False,
    )
```

time: 16.5 us -> 14.2 us (0.86)
  Pallas kernels: 15.4 us -> 13.1 us
  other arithmetic: 0.98 us -> 0 us
  local copies, waits for them, and re-layouts: 0 us -> 0.88 us
    pallas_call x1, Pallas kernels: 15.4 us -> 13.1 us  [local(): pl.pallas_call(functools.partial(kernel, sizes, groups, slots, scale), ou...]
    convert_element_type x1 -> x0, other arithmetic: 0.98 us -> none  [local(): return out.astype(BF16).reshape(3, elements, per, levels)]
    unnamed x0 -> x1, local copies, waits for them, and re-layouts: none -> 0.88 us
where the time goes in v1:
time: 14.2 us; the launch traced here: 14 us
  Pallas kernels  13.1 us (92%)
  local copies, waits for them, and re-layouts  0.88 us (6%)
    pallas_call x1, Pallas kernels, local(): pl.pallas_call(functools.partial(kernel, sizes, groups, slots, scale), ou...  13.1 us
    unnamed x1, local copies, waits for them, and re-layouts  0.88 us

profile of v1, /device:TPU:0, one launch (start us, length us, event | category | flops | bytes accessed | tf_op | source)
XLA Modules:
  0.0 14.0 jit_solution(7154128159049018214)
XLA Ops:
  0.0 13.1 %shard_map.73 = bf16[3,1024,128]{2,1,0:T(8,128)(2,1)S(1)} custom-call(bf16[3,1024,128]{2,1,0:T(8,128)(2,1)} %bitcast.8, f32[4,16,64]{2,1,0:T(8,128)} %bitcast.9, f32[16,64]{1,0:T(8,128)} %bitcast.10, s32[16,64]{1,0:T(8,128)} %bitcast.11, s32[1,212]{1,0:T(1,128)} %bitcast.12, s32[1,212]{1,0:T(1,128)} %bitcast.13, bf16[32,128]{1,0:T(8,128)(2,1)} %constant.2.clone.ops_hbm), custom_call_target="tpu_custom_call" | custom-call | tf_op jit(solution)/shard_map/pallas_call | solution.py:394
  13.1 0.9 %copy.9 = bf16[3,64,16,128]{3,2,1,0:T(8,128)(2,1)} copy(bf16[3,64,16,128]{3,2,1,0:T(8,128)(2,1)S(1)} %bitcast.7) | data formatting | bytes 1572864

commit v2 on v1

--- a/solution.py
+++ b/solution.py
@@ -17,6 +17,8 @@
 LANES = 128
 BULK = (2, 3)
 SMALL = (0, 1, 4, 5, 6, 7)
+LATE = ((2,), (0, 1, 4, 6), (3,), (1, 5, 7))
+GREETED = (1, 1, 0, 2, 1, 3, 1, 3)
 F32 = jnp.float32
 BF16 = jnp.bfloat16
 MESH = pl.DeviceIdType.MESH
@@ -127,7 +129,8 @@
     loads = [load(src, dst, k) for k, (src, dst) in enumerate((
         (metric_hbm, metric), (cor_hbm, cor), (node_hbm, node),
         (send_hbm, sendp), (recv_hbm, recvp), (ops_hbm, ops)))]
-    fields = [load(prog_hbm.at[f], prog.at[f], len(loads) + f) for f in range(3)]
+    for f in range(3):
+        load(prog_hbm.at[f], prog.at[f], 6)
 
     pl.semaphore_signal(mark, 1)
     me = lax.axis_index("face") * nsub + lax.axis_index("sub")
@@ -145,20 +148,21 @@
         first_lap.append(other < lap)
     higher = [jnp.logical_not(flag) for flag in lower]
     middle = lower[3] & higher[2]
+    turned = me == 0
+    later = lax.rem(me // nsub, 2) == 1
+    sooner = jnp.logical_not(later)
 
     barrier = pltpu.get_barrier_semaphore()
     for k, peer in enumerate(peers):
         @pl.when(higher[k])
         def _(peer=peer):
             pl.semaphore_signal(barrier, inc=1, device_id=peer, device_id_type=MESH)
-    for k, (_, _, used, first_row, padded) in enumerate(groups):
-        if k in BULK:
-            gap = pl.ds(first_row + used, padded - used)
-            arrived[0:2, gap] = jnp.zeros((2, padded - used, arrived.shape[2]), F32)
+    for _, _, used, first_row, padded in groups:
+        gap = pl.ds(first_row + used, padded - used)
+        arrived[0:2, gap] = jnp.zeros((2, padded - used, arrived.shape[2]), F32)
         if padded > used + 1:
             gap = pl.ds(first_row + used + 1, padded - used - 1)
-            part = slice(2, 3) if k in BULK else slice(0, 3)
-            arrived[part, gap] = jnp.zeros((part.stop - part.start, padded - used - 1, arrived.shape[2]), F32)
+            arrived[2:3, gap] = jnp.zeros((1, padded - used - 1, arrived.shape[2]), F32)
 
     expand[...] = jnp.where(
         iota((elements, nodes), 0) == iota((elements, nodes), 1) >> 4, 1.0, 0.0).astype(BF16)
@@ -220,8 +224,7 @@
         wide[0, rows] = first[:, :LANES]
         weighted[3, rows] = first[:, LANES:].astype(BF16)
 
-    for copy in fields:
-        copy.wait()
+    wait_bytes(prog, in_sem.at[6])
 
     diagonal = jnp.where(iota((BAND, BAND), 0) >> 4 == iota((BAND, BAND), 1) >> 4, 1.0, 0.0).astype(BF16)
 
@@ -252,17 +255,14 @@
         rows = pl.ds(groups[k][3], groups[k][2] + extra)
         return pltpu.make_async_remote_copy(
             src_ref=outgoing.at[part, rows], dst_ref=arrived.at[part, rows],
-            send_sem=send_sem.at[sem], recv_sem=recv_sem.at[sem],
+            send_sem=send_sem, recv_sem=recv_sem.at[sem],
             device_id=peers[k], device_id_type=MESH)
 
     def one_field(k):
-        return copy(k, pl.ds(2, 1), 1, 0)
+        return copy(k, pl.ds(2, 1), 1, 2 if k == 2 else 0)
 
     def two_fields(k):
         return copy(k, pl.ds(0, 2), 0, 1)
-
-    def all_fields(k):
-        return copy(k, pl.ds(0, 3), 1, 2 + SMALL.index(k))
 
     def early(copies, flag):
         @pl.when(flag)
@@ -270,12 +270,17 @@
             for item in copies:
                 item.start()
 
-    def late(copies, k):
-        @pl.when(higher[k])
+    def late(sem, k):
+        if k != 1:
+            return higher[k]
+        return higher[k] & (turned if sem == 3 else jnp.logical_not(turned))
+
+    def answered(sem):
+        count = sum(late(sem, k).astype(jnp.int32) for k in LATE[sem])
+
+        @pl.when(count > 0)
         def _():
-            pl.semaphore_wait(ready.at[k], 1)
-            for item in copies:
-                item.start()
+            pl.semaphore_wait(ready.at[sem], count)
 
     near_two, slot_mass = slot_sum(2, 3)
     outgoing[2] = near_two
@@ -291,10 +296,15 @@
 
     early([one_field(2)], lower[2])
     early([one_field(3)], middle)
+    for k in SMALL:
+        early([one_field(k)], lower[k])
     for k, peer in enumerate(peers):
-        @pl.when(lower[k])
-        def _(k=k, peer=peer):
-            pl.semaphore_signal(ready.at[k ^ 1], inc=1, device_id=peer, device_id_type=MESH)
+        other_last = me == total - 1
+        for sem, flag in ((GREETED[k ^ 1], lower[k]),) if k else (
+                (1, lower[k] & jnp.logical_not(other_last)), (3, lower[k] & other_last)):
+            @pl.when(flag)
+            def _(peer=peer, sem=sem):
+                pl.semaphore_signal(ready.at[sem], inc=1, device_id=peer, device_id_type=MESH)
 
     for band in range(nodes // BAND):
         rows = pl.ds(band * BAND, BAND)
@@ -309,41 +319,53 @@
     outgoing[0] = near_zero
     outgoing[1] = near_one
     for k in SMALL:
-        early([all_fields(k)], lower[k])
-    early([two_fields(2)], lower[2])
-    early([two_fields(3)], first_lap[3] & lower[3])
-    early([one_field(3), two_fields(3)], lower[3] & lower[2])
-    late([one_field(2)], 2)
-    for k in (0, 6, 4):
-        late([all_fields(k)], k)
-    early([two_fields(2)], higher[2])
-
+        early([two_fields(k)], lower[k])
+    early([two_fields(2)], lower[2] & sooner)
+    early([two_fields(3)], first_lap[3] & lower[3] & sooner)
     recv_col = jnp.sum(jnp.where(chosen, recvp[...].astype(F32), 0.0), axis=1, keepdims=True) + vacant
     same = iota((slots, slots), 0) == iota((slots, slots), 1)
     recv_row = jnp.sum(jnp.where(same, recv_col, 0.0), axis=0, keepdims=True)
     wide[1] = dot(spread[...], pick[:, 2 * LANES:])
     all_weighted = jnp.concatenate([weighted[f] for f in range(4)], axis=1)
-    for block in range(blocks):
-        rows = pl.ds(block * ROWS, ROWS)
-        point = wide[1, rows][:, 0:1]
-        meet = jnp.where(point == point_row, 1.0, 0.0).astype(BF16)
-        summed[rows, :] = dot(meet, all_weighted)
-
+    def gather_own(first, last):
+        for block_at in range(first, last):
+            rows = pl.ds(block_at * ROWS, ROWS)
+            point = wide[1, rows][:, 0:1]
+            meet = jnp.where(point == point_row, 1.0, 0.0).astype(BF16)
+            summed[rows, :] = dot(meet, all_weighted)
+            table_r[rows, :] = jnp.where(point == recv_row, 1.0, 0.0).astype(BF16)
+
+    gather_own(0, blocks // 2)
+    early([two_fields(2)], lower[2] & later)
+    answered(0)
+    early([one_field(2)], higher[2])
+    answered(1)
+    for k in LATE[1]:
+        early([one_field(k), two_fields(k)], late(1, k))
+    early([two_fields(2)], higher[2])
+    gather_own(blocks // 2, blocks)
+    early([two_fields(3)], first_lap[3] & lower[3] & later)
+    early([one_field(3), two_fields(3)], lower[3] & lower[2])
+    answered(2)
+    early([one_field(3)], higher[3])
+    answered(3)
+    for k in LATE[3]:
+        early([one_field(k), two_fields(k)], late(3, k))
+    early([two_fields(3)], higher[3])
+
+    rows_one = sum(group[2] + 1 for group in groups)
+    rows_up = groups[2][2] + 1
+    rows_two = sum(group[2] for group in groups)
+
+    def landing(sem):
+        wait_bytes((
+            arrived.at[pl.ds(2, 1), pl.ds(0, rows_one - rows_up)],
+            arrived.at[pl.ds(0, 2), pl.ds(0, rows_two)],
+            arrived.at[pl.ds(2, 1), pl.ds(0, rows_up)])[sem], recv_sem.at[sem])
+
+    landing(2)
     early([two_fields(3)], middle & jnp.logical_not(first_lap[3]))
-    for k in (1, 5, 7, 3):
-        late([one_field(k), two_fields(k)] if k in BULK else [all_fields(k)], k)
-
-    def landing(ref, sem):
-        rows_one = sum(groups[k][2] + 1 for k in BULK)
-        wait_bytes([
-            ref.at[pl.ds(2, 1), pl.ds(0, rows_one)],
-            ref.at[pl.ds(0, 2), pl.ds(0, rows_one - 2)],
-            *(ref.at[pl.ds(0, 3), pl.ds(0, groups[k][2] + 1)] for k in SMALL),
-        ][sem], (send_sem if ref is outgoing else recv_sem).at[sem])
-
-    landing(arrived, 0)
-    for k in (5, 7, 1, 6, 4, 0):
-        landing(arrived, 2 + SMALL.index(k))
+    landing(0)
     sides = [jnp.zeros((1, LANES), F32)] * (slots // LANES)
     for _, _, used, first_row, _ in groups:
         sides[first_row // LANES] += arrived[2, first_row + used:first_row + used + 1]
@@ -351,18 +373,12 @@
     ones = jnp.ones((slots, LANES), BF16)
     for block in range(blocks):
         rows = pl.ds(block * ROWS, ROWS)
-        point = wide[1, rows][:, 0:1]
-        hit = point == recv_row
-        table_r[rows, :] = jnp.where(hit, 1.0, 0.0).astype(BF16)
-        far = dot(jnp.where(hit, mass_in, 0.0).astype(BF16), ones)
+        far = dot(table_r[rows, :] * mass_in.astype(BF16), ones)
         inv = (STEP_SIZE / scale) / (summed[rows, 3 * LANES:] + far)
         inverse[rows, :] = inv
         for f in range(3):
             lanes = slice(f * LANES, (f + 1) * LANES)
             summed[rows, lanes] = prog[f, rows].astype(F32) + inv * summed[rows, lanes]
-
-    for sem in range(2, 2 + len(SMALL)):
-        landing(outgoing, sem)
 
     def finish(chosen_fields):
         landed = jnp.concatenate([arrived[f].astype(BF16) for f in chosen_fields], axis=1)
@@ -374,10 +390,9 @@
                 out_hbm[f, rows] = value.astype(out_hbm.dtype)
 
     finish([2])
-    landing(arrived, 1)
+    landing(1)
     finish([0, 1])
-    for sem in range(2):
-        landing(outgoing, sem)
+    wait_bytes(wide.at[0, pl.ds(0, rows_one + 2 * rows_two)], send_sem)
     pl.semaphore_wait(mark, 1)
 
 
@@ -417,10 +432,10 @@
             vmem((64, nodes), BF16),
             vmem((3, slots, levels), F32),
             vmem((3, slots, levels), F32),
-            dma((9,)),
-            dma((2 + len(SMALL),)),
-            dma((2 + len(SMALL),)),
-            pltpu.SemaphoreType.REGULAR((len(groups),)),
+            dma((7,)),
+            dma,
+            dma((3,)),
+            pltpu.SemaphoreType.REGULAR((4,)),
             pltpu.SemaphoreType.REGULAR,
         ],
         compiler_params=pltpu.CompilerParams(

time: 14.2 us -> 13.6 us (0.958)
  Pallas kernels: 13.1 us -> 12.4 us
    pallas_call x1, Pallas kernels: 13.1 us -> 12.4 us  [local(): pl.pallas_call(functools.partial(kernel, sizes, groups, slots, scale), ou...]
where the time goes in v2:
time: 13.6 us; the launch traced here: 13.3 us
  Pallas kernels  12.4 us (91%)
  local copies, waits for them, and re-layouts  0.88 us (6%)
    pallas_call x1, Pallas kernels, local(): pl.pallas_call(functools.partial(kernel, sizes, groups, slots, scale), ou...  12.4 us
    unnamed x1, local copies, waits for them, and re-layouts  0.88 us

profile of v2, /device:TPU:0, one launch (start us, length us, event | category | flops | bytes accessed | tf_op | source)
XLA Modules:
  0.0 13.3 jit_solution(18401763503025365271)
XLA Ops:
  0.0 12.4 %shard_map.73 = bf16[3,1024,128]{2,1,0:T(8,128)(2,1)S(1)} custom-call(bf16[3,1024,128]{2,1,0:T(8,128)(2,1)} %bitcast.8, f32[4,16,64]{2,1,0:T(8,128)} %bitcast.9, f32[16,64]{1,0:T(8,128)} %bitcast.10, s32[16,64]{1,0:T(8,128)} %bitcast.11, s32[1,212]{1,0:T(1,128)} %bitcast.12, s32[1,212]{1,0:T(1,128)} %bitcast.13, bf16[32,128]{1,0:T(8,128)(2,1)} %constant.2.clone.ops_hbm), custom_call_target="tpu_custom_call" | custom-call | tf_op jit(solution)/shard_map/pallas_call | solution.py:409
  12.4 0.9 %copy.9 = bf16[3,64,16,128]{3,2,1,0:T(8,128)(2,1)} copy(bf16[3,64,16,128]{3,2,1,0:T(8,128)(2,1)S(1)} %bitcast.7) | data formatting | bytes 1572864

commit v3 on v2

--- a/solution.py
+++ b/solution.py
@@ -109,9 +109,9 @@
 def kernel(
     sizes, groups, slots, scale,
     prog_hbm, metric_hbm, cor_hbm, node_hbm, send_hbm, recv_hbm, ops_hbm,
-    out_hbm,
+    done, base, inverse, table_r, landed,
     prog, metric, cor, node, sendp, recvp, ops,
-    wide, weighted, summed, inverse, table_s, table_r,
+    wide, weighted, summed, table_s,
     expand, pick, spread, vort, slim,
     outgoing, arrived, in_sem, send_sem, recv_sem, ready, mark,
 ):
@@ -149,6 +149,7 @@
     higher = [jnp.logical_not(flag) for flag in lower]
     middle = lower[3] & higher[2]
     turned = me == 0
+    crossing = higher[5] & lower[3]
     later = lax.rem(me // nsub, 2) == 1
     sooner = jnp.logical_not(later)
 
@@ -224,6 +225,28 @@
         wide[0, rows] = first[:, :LANES]
         weighted[3, rows] = first[:, LANES:].astype(BF16)
 
+    waited = sum(flag.astype(jnp.int32) for flag in lower)
+    prompt = (me == total - 1) | (me == total - lap + 1)
+
+    def enter():
+        @pl.when(waited > 0)
+        def _():
+            pl.semaphore_wait(barrier, waited)
+
+    def reply(flag):
+        other_last = me == total - 1
+        for k, peer in enumerate(peers):
+            for sem, which in ((GREETED[k ^ 1], lower[k]),) if k else (
+                    (1, lower[k] & jnp.logical_not(other_last)), (3, lower[k] & other_last)):
+                @pl.when(flag & which)
+                def _(peer=peer, sem=sem):
+                    pl.semaphore_signal(ready.at[sem], inc=1, device_id=peer, device_id_type=MESH)
+
+    @pl.when(prompt)
+    def _():
+        enter()
+        reply(True)
+
     wait_bytes(prog, in_sem.at[6])
 
     diagonal = jnp.where(iota((BAND, BAND), 0) >> 4 == iota((BAND, BAND), 1) >> 4, 1.0, 0.0).astype(BF16)
@@ -288,23 +311,15 @@
     for _, _, used, first_row, size in groups:
         outgoing[2, first_row + used:first_row + used + 1] = jnp.sum(
             place[first_row:first_row + size], axis=0, keepdims=True)
-    waited = sum(flag.astype(jnp.int32) for flag in lower)
-
-    @pl.when(waited > 0)
+    @pl.when(jnp.logical_not(prompt))
     def _():
-        pl.semaphore_wait(barrier, waited)
+        enter()
 
     early([one_field(2)], lower[2])
     early([one_field(3)], middle)
     for k in SMALL:
         early([one_field(k)], lower[k])
-    for k, peer in enumerate(peers):
-        other_last = me == total - 1
-        for sem, flag in ((GREETED[k ^ 1], lower[k]),) if k else (
-                (1, lower[k] & jnp.logical_not(other_last)), (3, lower[k] & other_last)):
-            @pl.when(flag)
-            def _(peer=peer, sem=sem):
-                pl.semaphore_signal(ready.at[sem], inc=1, device_id=peer, device_id_type=MESH)
+    reply(jnp.logical_not(prompt))
 
     for band in range(nodes // BAND):
         rows = pl.ds(band * BAND, BAND)
@@ -339,10 +354,11 @@
     early([two_fields(2)], lower[2] & later)
     answered(0)
     early([one_field(2)], higher[2])
+    early([two_fields(2)], higher[2] & higher[3])
     answered(1)
     for k in LATE[1]:
         early([one_field(k), two_fields(k)], late(1, k))
-    early([two_fields(2)], higher[2])
+    early([two_fields(2)], higher[2] & lower[3] & jnp.logical_not(crossing))
     gather_own(blocks // 2, blocks)
     early([two_fields(3)], first_lap[3] & lower[3] & later)
     early([one_field(3), two_fields(3)], lower[3] & lower[2])
@@ -351,7 +367,8 @@
     answered(3)
     for k in LATE[3]:
         early([one_field(k), two_fields(k)], late(3, k))
-    early([two_fields(3)], higher[3])
+    early([two_fields(2)], crossing)
+    early([two_fields(3)], higher[3] & sooner)
 
     rows_one = sum(group[2] + 1 for group in groups)
     rows_up = groups[2][2] + 1
@@ -364,6 +381,7 @@
             arrived.at[pl.ds(2, 1), pl.ds(0, rows_up)])[sem], recv_sem.at[sem])
 
     landing(2)
+    early([two_fields(3)], higher[3] & later)
     early([two_fields(3)], middle & jnp.logical_not(first_lap[3]))
     landing(0)
     sides = [jnp.zeros((1, LANES), F32)] * (slots // LANES)
@@ -378,22 +396,38 @@
         inverse[rows, :] = inv
         for f in range(3):
             lanes = slice(f * LANES, (f + 1) * LANES)
-            summed[rows, lanes] = prog[f, rows].astype(F32) + inv * summed[rows, lanes]
-
-    def finish(chosen_fields):
-        landed = jnp.concatenate([arrived[f].astype(BF16) for f in chosen_fields], axis=1)
+            start = prog[f, rows].astype(F32) + inv * summed[rows, lanes]
+            if f == 2:
+                summed[rows, lanes] = start
+            else:
+                base[f, rows] = start
+
+    def finish():
+        last = arrived[2].astype(BF16)
         for block_at in range(blocks):
             rows = pl.ds(block_at * ROWS, ROWS)
-            far = dot(table_r[rows, :], landed)
-            for j, f in enumerate(chosen_fields):
-                value = summed[rows, f * LANES:(f + 1) * LANES] + inverse[rows, :] * far[:, j * LANES:(j + 1) * LANES]
-                out_hbm[f, rows] = value.astype(out_hbm.dtype)
-
-    finish([2])
+            far = dot(table_r[rows, :], last)
+            done[rows, :] = (summed[rows, 2 * LANES:3 * LANES] + inverse[rows, :] * far).astype(BF16)
+
+    finish()
     landing(1)
-    finish([0, 1])
+    for f in range(2):
+        landed[f] = arrived[f].astype(BF16)
     wait_bytes(wide.at[0, pl.ds(0, rows_one + 2 * rows_two)], send_sem)
     pl.semaphore_wait(mark, 1)
+
+
+def closing(done, base, inverse, table_r, landed, out_hbm, fresh, sem):
+    nodes = done.shape[0]
+    pltpu.make_async_copy(done, out_hbm.at[2], sem).start()
+    far_in = jnp.concatenate([landed[0], landed[1]], axis=1)
+    for block_at in range(nodes // ROWS):
+        rows = pl.ds(block_at * ROWS, ROWS)
+        far = dot(table_r[rows, :], far_in)
+        for f in range(2):
+            fresh[f, rows] = (base[f, rows] + inverse[rows, :] * far[:, f * LANES:(f + 1) * LANES]).astype(BF16)
+        pltpu.make_async_copy(fresh.at[:, rows], out_hbm.at[pl.ds(0, 2), rows], sem).start()
+    wait_bytes(out_hbm, sem)
 
 
 def local(prognostic, metric, coriolis, node_point, send_point, recv_point):
@@ -406,11 +440,13 @@
     any_spec = pl.BlockSpec(memory_space=pltpu.HBM)
     dma = pltpu.SemaphoreType.DMA
     vmem = pltpu.VMEM
-    out = pl.pallas_call(
+    held = pl.pallas_call(
         functools.partial(kernel, sizes, groups, slots, scale),
-        out_shape=pltpu.VMEM((3, nodes, levels), BF16),
+        out_shape=(
+            vmem((nodes, levels), BF16), vmem((2, nodes, levels), F32), vmem((nodes, levels), F32),
+            vmem((nodes, slots), BF16), vmem((2, slots, levels), BF16)),
         in_specs=[any_spec] * 7,
-        out_specs=pl.BlockSpec(memory_space=pltpu.VMEM),
+        out_specs=[pl.BlockSpec(memory_space=pltpu.VMEM)] * 5,
         scratch_shapes=[
             vmem((3, nodes, levels), BF16),
             vmem((4, per, elements), F32),
@@ -422,9 +458,7 @@
             vmem((2, nodes, LANES), F32),
             vmem((4, nodes, LANES), BF16),
             vmem((nodes, 4 * LANES), F32),
-            vmem((nodes, LANES), F32),
             vmem((slots, nodes), BF16),
-            vmem((nodes, slots), BF16),
             vmem((elements, nodes), BF16),
             vmem((LANES, 3 * LANES), BF16),
             vmem((nodes, LANES), BF16),
@@ -445,6 +479,14 @@
         send_point.reshape(1, links), recv_point.reshape(1, links),
         jnp.asarray(tables, dtype=BF16),
     )
+    out = pl.pallas_call(
+        closing,
+        out_shape=jax.ShapeDtypeStruct((3, nodes, levels), BF16),
+        in_specs=[pl.BlockSpec(memory_space=pltpu.VMEM)] * 5,
+        out_specs=any_spec,
+        scratch_shapes=[vmem((2, nodes, levels), BF16), dma],
+        compiler_params=pltpu.CompilerParams(vmem_limit_bytes=8 * 1024 * 1024),
+    )(*[pltpu.with_memory_space_constraint(part, pltpu.VMEM) for part in held])
     return out.reshape(3, elements, per, levels)
 
 

time: 13.6 us -> 13.3 us (0.978)
  the two profiles are of different devices: /device:TPU:0 before, /device:TPU:1 now
where the time goes in v3:
time: 13.3 us; the launch traced here: 13.2 us
  Pallas kernels  13.2 us (99%)
    pallas_call x1, Pallas kernels, local(): pl.pallas_call(functools.partial(kernel, sizes, groups, slots, scale), ou...  12.1 us
    pallas_call x1, Pallas kernels, local(): pl.pallas_call(closing, out_shape=jax.ShapeDtypeStruct((3, nodes, levels)...  1.03 us

profile of v3, /device:TPU:1, one launch (start us, length us, event | category | flops | bytes accessed | tf_op | source)
XLA Modules:
  0.0 13.2 jit_solution(2852994294639367146)
XLA Ops:
  0.0 12.1 %shard_map.73 = (bf16[1024,128]{1,0:T(8,128)(2,1)S(1)}, f32[2,1024,128]{2,1,0:T(8,128)S(1)}, f32[1024,128]{1,0:T(8,128)S(1)}, bf16[1024,256]{1,0:T(8,128)(2,1)S(1)}, bf16[2,256,128]{2,1,0:T(8,128)(2,1)S(1)}) custom-call(bf16[3,1024,128]{2,1,0:T(8,128)(2,1)} %bitcast.7, f32[4,16,64]{2,1,0:T(8,128)} %bitcast.8, f32[16,64]{1,0:T(8,128)} %bitcast.9, ...), custom_call_target="tpu_custom_call" | custom-call | tf_op jit(solution)/shard_map/pallas_call | solution.py:443
  12.2 1.0 %shard_map.74 = bf16[3,1024,128]{2,1,0:T(8,128)(2,1)} custom-call(bf16[1024,128]{1,0:T(8,128)(2,1)S(1)} %get-tuple-element.10.done, f32[2,1024,128]{2,1,0:T(8,128)S(1)} %get-tuple-element.11.base, f32[1024,128]{1,0:T(8,128)S(1)} %get-tuple-element.12.inverse, bf16[1024,256]{1,0:T(8,128)(2,1)S(1)} %get-tuple-element.13.table_r, ...), custom_call_target="tpu_custom_call" | custom-call | tf_op jit(solution)/shard_map/pallas_call | solution.py:482

commit v4 on v3

--- a/solution.py
+++ b/solution.py
@@ -421,8 +421,8 @@
     nodes = done.shape[0]
     pltpu.make_async_copy(done, out_hbm.at[2], sem).start()
     far_in = jnp.concatenate([landed[0], landed[1]], axis=1)
-    for block_at in range(nodes // ROWS):
-        rows = pl.ds(block_at * ROWS, ROWS)
+    for block_at in range(nodes // BAND):
+        rows = pl.ds(block_at * BAND, BAND)
         far = dot(table_r[rows, :], far_in)
         for f in range(2):
             fresh[f, rows] = (base[f, rows] + inverse[rows, :] * far[:, f * LANES:(f + 1) * LANES]).astype(BF16)

time: 13.3 us -> 13.3 us (level)
  no operation moved by 1% of the time
where the time goes in v4:
time: 13.3 us; the launch traced here: 13.1 us
  Pallas kernels  13.1 us (98%)
    pallas_call x1, Pallas kernels, local(): pl.pallas_call(functools.partial(kernel, sizes, groups, slots, scale), ou...  12.1 us
    pallas_call x1, Pallas kernels, local(): pl.pallas_call(closing, out_shape=jax.ShapeDtypeStruct((3, nodes, levels)...  1 us

profile of v4, /device:TPU:1, one launch (start us, length us, event | category | flops | bytes accessed | tf_op | source)
XLA Modules:
  0.0 13.1 jit_solution(16690250416258430150)
XLA Ops:
  0.0 12.1 %shard_map.73 = (bf16[1024,128]{1,0:T(8,128)(2,1)S(1)}, f32[2,1024,128]{2,1,0:T(8,128)S(1)}, f32[1024,128]{1,0:T(8,128)S(1)}, bf16[1024,256]{1,0:T(8,128)(2,1)S(1)}, bf16[2,256,128]{2,1,0:T(8,128)(2,1)S(1)}) custom-call(bf16[3,1024,128]{2,1,0:T(8,128)(2,1)} %bitcast.7, f32[4,16,64]{2,1,0:T(8,128)} %bitcast.8, f32[16,64]{1,0:T(8,128)} %bitcast.9, ...), custom_call_target="tpu_custom_call" | custom-call | tf_op jit(solution)/shard_map/pallas_call | solution.py:443
  12.2 1.0 %shard_map.74 = bf16[3,1024,128]{2,1,0:T(8,128)(2,1)} custom-call(bf16[1024,128]{1,0:T(8,128)(2,1)S(1)} %get-tuple-element.10.done, f32[2,1024,128]{2,1,0:T(8,128)S(1)} %get-tuple-element.11.base, f32[1024,128]{1,0:T(8,128)S(1)} %get-tuple-element.12.inverse, bf16[1024,256]{1,0:T(8,128)(2,1)S(1)} %get-tuple-element.13.table_r, ...), custom_call_target="tpu_custom_call" | custom-call | tf_op jit(solution)/shard_map/pallas_call | solution.py:482
